TPU v7x, 32 devices: a whole 2x2x4 slice. The times are simulated.
32 devices in a mesh: lat: 8 (over z, x), lon: 4 (over y, core).
Axes of the slice: x: 2, y: 2, z: 4, core: 2. Of those that a mesh axis runs over, the one named last changes fastest.
Arguments:
- fields: float32 [8, 8, 128, 512], P(None, None, 'lat', 'lon'), may hold values from -6 to 6
- ocean_mask: int32 [128, 4], replicated, may hold values from 0 to 1, as said below
- scale_table: float32 [16], replicated, may hold values from 0.5 to 4
- offset_table: float32 [16], replicated, may hold values from -4 to 4
- scale_index: int32 [8], replicated, may hold values from 0 to 15
- offset_index: int32 [8], replicated, may hold values from 0 to 15
Outputs:
- history: float32 [8, 8, 128, 512], P(None, 'lat', 'lon')
- record_range: float32 [2, 8, 8], P(None, None, 'lat')
Inputs may be any that keep to these rules, and one draw needn't show every extreme that they name: `ocean_mask`: each device's block of 16 rows and 128 longitudes holds at least half of 12 (rounded down, and never fewer than one) and at most 12 ocean strips; some block holds exactly 12.
All inputs are finite; a program needn't handle non-finite values.
Results may differ from a plain program's by a relative error of at most 0.00007.
Values sent between devices are 32-bit elements; how exact they have to be, the bound alone decides.
A program may use at most 64 MiB of HBM per device.

v0:
```python
import jax
import jax.numpy as jnp
from jax import lax
from jax.sharding import PartitionSpec as P

STRIP = 128


def per_device(fields, ocean_mask, scale_table, offset_table, scale_index, offset_index):
    nfield, level_count, lat_rows, lon_cells = fields.shape
    lat_count = lax.axis_size("lat")
    lon_count = lax.axis_size("lon")
    lat_pos = lax.axis_index("lat")
    lon_pos = lax.axis_index("lon")
    strips = lon_cells // STRIP
    slab_blocks = lat_count // lon_count
    table_slots = jnp.arange(scale_table.shape[0])
    scale_pick = scale_index[:, None] == table_slots[None, :]
    offset_pick = offset_index[:, None] == table_slots[None, :]
    scales = jnp.sum(jnp.where(scale_pick, scale_table[None, :], 0.0), axis=1)
    offsets = jnp.sum(jnp.where(offset_pick, offset_table[None, :], 0.0), axis=1)
    own_mask = lax.dynamic_slice(
        ocean_mask, (lat_pos * lat_rows, lon_pos * strips), (lat_rows, strips)
    )
    own_live = jnp.repeat(own_mask, STRIP, axis=1) > 0
    packed = (fields - offsets[:, None, None, None]) * scales[:, None, None, None]
    slab_mask = lax.dynamic_slice(
        ocean_mask,
        (lon_pos * slab_blocks * lat_rows, 0),
        (slab_blocks * lat_rows, lon_count * strips),
    )
    slab_live = jnp.repeat(slab_mask, STRIP, axis=1) > 0
    masked_block = jnp.where(own_live[None, None], packed, 0.0)
    history = lax.all_to_all(
        lax.all_to_all(masked_block, "lat", split_axis=1, concat_axis=2, tiled=True),
        "lon",
        split_axis=2,
        concat_axis=3,
        tiled=True,
    )
    highest = jnp.max(jnp.where(slab_live[None, None], history, -jnp.inf), axis=(2, 3))
    negated = jnp.max(jnp.where(slab_live[None, None], -history, -jnp.inf), axis=(2, 3))
    own_levels = lax.pmax(jnp.stack([highest, negated]), "lon")
    record_range = jnp.stack([own_levels[0], -own_levels[1]])
    return (history, record_range)


def solution(mesh):
    return jax.shard_map(
        per_device,
        mesh=mesh,
        in_specs=(P(None, None, "lat", "lon"), P(), P(), P(), P(), P()),
        out_specs=(P(None, "lat", "lon", None), P(None, None, "lat")),
        check_vma=False,
    )
```

profile of v0, /device:TPU:0, one launch (start us, length us, event | category | flops | bytes accessed | tf_op | source)
XLA Modules:
  0.0 46.4 jit_solution(1260978863947469488)
XLA Ops:
  0.6 0.0 copy-start
  0.6 0.7 %copy-done = s32[128,4]{0,1:T(4,128)S(1)} copy-done((s32[128,4]{0,1:T(4,128)S(1)}, s32[128,4]{0,1:T(4,128)}, u32[]{:S(2)}) %copy-start) | copy-done | bytes 2072
  1.3 0.0 copy-start.1
  1.3 0.0 copy-start.2
  1.3 0.0 copy-start.3
  1.3 0.0 copy-start.4
  1.3 0.1 compare_bitcast_fusion
  1.4 0.6 %copy-done.1 = f32[16]{0:T(128)S(1)} copy-done((f32[16]{0:T(128)S(1)}, f32[16]{0:T(128)}, u32[]{:S(2)}) %copy-start.1) | copy-done | bytes 88
  2.0 0.0 copy-done.2
  2.0 0.0 copy-done.3
  2.0 0.0 copy-done.4
  2.0 0.2 select_reduce_fusion.2
  2.2 1.3 %fusion.1 = f32[8,8,16,128]{3,2,0,1:T(8,128)S(1)} fusion(f32[8,8,16,128]{3,2,1,0:T(8,128)} %param.6, f32[8]{0:T(128)S(1)} %get-tuple-element.14, f32[8]{0:T(128)S(1)} %get-tuple-element.15, pred[16]{0:T(512)(128)(4,1)S(1)} %compare_bitcast_fusion), kind=kLoop, calls=%fused_computation.2 | loop fusion | flops 393216 | bytes 1048656 | tf_op jit(solution)/shard_map/jit(_where)/select_n | solution.py:33
  3.5 21.6 %all_to_all.30 = f32[8,8,16,128]{3,2,0,1:T(8,128)S(1)} all-to-all(f32[8,8,16,128]{3,2,0,1:T(8,128)S(1)} %fusion.1), channel_id=1, replica_groups=mesh['lat'=8,'lon'=4] {'lat'}, dimensions={1} | all-to-all | bytes 1048576 | tf_op jit(solution)/shard_map/all_to_all | solution.py:35
  25.2 1.1 %copy.23 = f32[8,1,128,128]{3,0,1,2:T(8,128)} copy(f32[8,1,128,128]{3,2,0,1:T(8,128)S(1)} %bitcast.12) | data formatting | bytes 1048576 | tf_op jit(solution)/shard_map/all_to_all | solution.py:35
  26.3 3.5 %all-to-all-start.1 = ((f32[8,1,128,128]{3,0,1,2:T(8,128)}), f32[8,1,128,128]{3,0,1,2:T(8,128)S(1)}, u32[]{:S(2)}, u32[]{:S(2)}) async-start(f32[8,1,128,128]{3,0,1,2:T(8,128)} %copy.23), calls=%async_computation.1 | async-start | bytes 1048576 | tf_op jit(solution)/shard_map/all_to_all | solution.py:34
  29.7 0.1 dynamic-slice_compare_fusion
  29.8 8.7 %all-to-all-done.1 = f32[8,1,128,128]{3,0,1,2:T(8,128)S(1)} async-done(((f32[8,1,128,128]{3,0,1,2:T(8,128)}), f32[8,1,128,128]{3,0,1,2:T(8,128)S(1)}, u32[]{:S(2)}, u32[]{:S(2)}) %all-to-all-start.1) | async-done | bytes 524320 | tf_op jit(solution)/shard_map/all_to_all | solution.py:34
  38.5 0.1 copy.24
  38.6 0.3 copy.25
  39.0 0.3 select_reduce_fusion.1
  39.3 0.8 %copy.26 = f32[8,1,32,512]{3,2,1,0:T(8,128)} copy(f32[8,1,32,512]{3,1,2,0:T(1,128)S(1)} %bitcast.11) | data formatting | bytes 1048576
  40.1 5.7 %pmax.7 = f32[2,8,1]{1,2,0:T(1,128)S(1)} all-reduce(f32[2,8,1]{1,2,0:T(1,128)S(1)} %pad_maximum_fusion), channel_id=1, replica_groups=mesh['lat'=8,'lon'=4] {'lon'}, use_global_device_ids=true, to_apply=%region_4.5 | all-reduce | flops 16 | bytes 128 | tf_op jit(solution)/shard_map/pmax | solution.py:43
  45.9 0.6 %pad_maximum_fusion.1 = f32[2,8,1]{1,2,0:T(1,128)} fusion(f32[1,8,1]{1,2,0:T(1,128)S(1)} %get-tuple-element.13, f32[1,8,1]{1,2,0:T(1,128)S(1)} %get-tuple-element.12), kind=kLoop, calls=%fused_computation.12 | loop fusion | flops 16 | bytes 128 | tf_op jit(solution)/shard_map/stack | solution.py:44
  (3 shorter events, 0.1 us)
Async XLA Ops:
  0.6 0.7 %copy-start = (s32[128,4]{0,1:T(4,128)S(1)}, s32[128,4]{0,1:T(4,128)}, u32[]{:S(2)}) copy-start(s32[128,4]{0,1:T(4,128)} %param.7) | copy-start | bytes 6148
  1.3 0.7 %copy-start.1 = (f32[16]{0:T(128)S(1)}, f32[16]{0:T(128)}, u32[]{:S(2)}) copy-start(f32[16]{0:T(128)} %param.8) | copy-start | bytes 196
  1.3 0.7 %copy-start.2 = (s32[8]{0:T(128)S(1)}, s32[8]{0:T(128)}, u32[]{:S(2)}) copy-start(s32[8]{0:T(128)} %param.10) | copy-start | bytes 100
  1.3 0.7 %copy-start.3 = (f32[16]{0:T(128)S(1)}, f32[16]{0:T(128)}, u32[]{:S(2)}) copy-start(f32[16]{0:T(128)} %param.9) | copy-start | bytes 196
  1.3 0.7 %copy-start.4 = (s32[8]{0:T(128)S(1)}, s32[8]{0:T(128)}, u32[]{:S(2)}) copy-start(s32[8]{0:T(128)} %param.11) | copy-start | bytes 100
  26.3 12.3 %all-to-all-start.1 = ((f32[8,1,128,128]{3,0,1,2:T(8,128)}), f32[8,1,128,128]{3,0,1,2:T(8,128)S(1)}, u32[]{:S(2)}, u32[]{:S(2)}) async-start(f32[8,1,128,128]{3,0,1,2:T(8,128)} %copy.23), calls=%async_computation.1 | async-start | bytes 1048576 | tf_op jit(solution)/shard_map/all_to_all | solution.py:34
where the time goes:
time: 46.7 us; the launch traced here: 46.4 us
  blocking collectives  27.3 us (58%)
  waiting for transfers between devices  8.7 us (19%)
  local copies, waits for them, and re-layouts  3.72 us (8%)
  starting transfers between devices  3.47 us (7%)
  other arithmetic  2.49 us (5%)
  between operations  0.7 us (1%)
    all_to_all x1, blocking collectives, per_device(): lax.all_to_all(masked_block, 'lat', split_axis=1, concat_axis=2, tiled=True)  21.6 us
    all_to_all x1, waiting for transfers between devices, per_device(): lax.all_to_all(lax.all_to_all(masked_block, 'lat', split_axis=1, concat_a...  8.7 us
    pmax x1, blocking collectives, per_device(): own_levels = lax.pmax(jnp.stack([highest, negated]), 'lon')  5.74 us
    all_to_all x1, starting transfers between devices, per_device(): lax.all_to_all(lax.all_to_all(masked_block, 'lat', split_axis=1, concat_a...  3.47 us
    unnamed x11, local copies, waits for them, and re-layouts  2.14 us
    select_n x1, other arithmetic, per_device(): masked_block = jnp.where(own_live[None, None], packed, 0.0)  1.26 us
    all_to_all x2, local copies, waits for them, and re-layouts, per_device(): lax.all_to_all(masked_block, 'lat', split_axis=1, concat_axis=2, tiled=True)  1.14 us
  transfers between devices with their start and end apart: 1, of which 1 were waited for; matrix products, arithmetic and copies ran while one was open for 0% of the time, Pallas kernels for 0%

commit v1 on v0

--- a/solution.py
+++ b/solution.py
@@ -31,12 +31,20 @@
     )
     slab_live = jnp.repeat(slab_mask, STRIP, axis=1) > 0
     masked_block = jnp.where(own_live[None, None], packed, 0.0)
-    history = lax.all_to_all(
-        lax.all_to_all(masked_block, "lat", split_axis=1, concat_axis=2, tiled=True),
-        "lon",
-        split_axis=2,
-        concat_axis=3,
-        tiled=True,
+    history = jnp.concatenate(
+        lax.all_to_all(
+            jnp.stack(
+                jnp.split(
+                    lax.all_to_all(masked_block, "lat", split_axis=1, concat_axis=2, tiled=True),
+                    lax.axis_size("lon"),
+                    axis=2,
+                )
+            ),
+            "lon",
+            0,
+            0,
+        ),
+        axis=3,
     )
     highest = jnp.max(jnp.where(slab_live[None, None], history, -jnp.inf), axis=(2, 3))
     negated = jnp.max(jnp.where(slab_live[None, None], -history, -jnp.inf), axis=(2, 3))

time: 46.7 us -> 46.4 us (level)
  local copies, waits for them, and re-layouts: 3.72 us -> 2.55 us
  other arithmetic: 2.49 us -> 3.32 us
    all_to_all x2 -> x1, local copies, waits for them, and re-layouts: 1.14 us -> 0.04 us  [per_device(): lax.all_to_all(masked_block, 'lat', split_axis=1, concat_axis=2, tiled=True)]
    another operation x0 -> x1, other arithmetic: none -> 0.83 us  [per_device(): jnp.stack(jnp.split(lax.all_to_all(masked_block, 'lat', split_axis=1, con...]
where the time goes in v1:
time: 46.4 us; the launch traced here: 46.1 us
  blocking collectives  27.4 us (59%)
  waiting for transfers between devices  8.7 us (19%)
  starting transfers between devices  3.47 us (7%)
  other arithmetic  3.32 us (7%)
  local copies, waits for them, and re-layouts  2.55 us (5%)
  between operations  0.7 us (2%)
    all_to_all x1, blocking collectives, per_device(): lax.all_to_all(masked_block, 'lat', split_axis=1, concat_axis=2, tiled=True)  21.6 us
    all_to_all x1, waiting for transfers between devices, per_device(): lax.all_to_all(jnp.stack(jnp.split(lax.all_to_all(masked_block, 'lat', sp...  8.7 us
    pmax x1, blocking collectives, per_device(): own_levels = lax.pmax(jnp.stack([highest, negated]), 'lon')  5.76 us
    all_to_all x1, starting transfers between devices, per_device(): lax.all_to_all(jnp.stack(jnp.split(lax.all_to_all(masked_block, 'lat', sp...  3.47 us
    unnamed x11, local copies, waits for them, and re-layouts  2.14 us
    select_n x1, other arithmetic, per_device(): masked_block = jnp.where(own_live[None, None], packed, 0.0)  1.26 us
  transfers between devices with their start and end apart: 1, of which 1 were waited for; matrix products, arithmetic and copies ran while one was open for 0% of the time, Pallas kernels for 0%

profile of v1, /device:TPU:0, one launch (start us, length us, event | category | flops | bytes accessed | tf_op | source)
XLA Modules:
  0.0 46.1 jit_solution(15658703029161010893)
XLA Ops:
  0.6 0.0 copy-start
  0.6 0.7 %copy-done = s32[128,4]{0,1:T(4,128)S(1)} copy-done((s32[128,4]{0,1:T(4,128)S(1)}, s32[128,4]{0,1:T(4,128)}, u32[]{:S(2)}) %copy-start) | copy-done | bytes 2072
  1.3 0.0 copy-start.1
  1.3 0.0 copy-start.2
  1.3 0.0 copy-start.3
  1.3 0.0 copy-start.4
  1.3 0.1 compare_bitcast_fusion
  1.4 0.6 %copy-done.1 = f32[16]{0:T(128)S(1)} copy-done((f32[16]{0:T(128)S(1)}, f32[16]{0:T(128)}, u32[]{:S(2)}) %copy-start.1) | copy-done | bytes 88
  2.0 0.0 copy-done.2
  2.0 0.0 copy-done.3
  2.0 0.0 copy-done.4
  2.0 0.2 select_reduce_fusion.2
  2.2 1.3 %fusion.1 = f32[8,8,16,128]{3,2,0,1:T(8,128)S(1)} fusion(f32[8,8,16,128]{3,2,1,0:T(8,128)} %param.6, f32[8]{0:T(128)S(1)} %get-tuple-element.14, f32[8]{0:T(128)S(1)} %get-tuple-element.15, pred[16]{0:T(512)(128)(4,1)S(1)} %compare_bitcast_fusion), kind=kLoop, calls=%fused_computation.3 | loop fusion | flops 393216 | bytes 1048656 | tf_op jit(solution)/shard_map/jit(_where)/select_n | solution.py:33
  3.5 21.6 %all_to_all.17 = f32[8,8,16,128]{3,2,0,1:T(8,128)S(1)} all-to-all(f32[8,8,16,128]{3,2,0,1:T(8,128)S(1)} %fusion.1), channel_id=1, replica_groups=mesh['lat'=8,'lon'=4] {'lat'}, dimensions={1} | all-to-all | bytes 1048576 | tf_op jit(solution)/shard_map/all_to_all | solution.py:38
  25.2 0.8 %pad_maximum_fusion = f32[4,8,1,32,128]{4,3,1,2,0:T(8,128)} fusion(f32[1,8,1,32,128]{4,3,1,2,0:T(8,128)S(1)} %get-tuple-element.9, f32[1,8,1,32,128]{4,3,1,2,0:T(8,128)S(1)} %get-tuple-element.10, f32[1,8,1,32,128]{4,3,1,2,0:T(8,128)S(1)} %get-tuple-element.11, f32[1,8,1,32,128]{4,3,1,2,0:T(8,128)S(1)} %get-tuple-element.8), kind=kLoop, calls=%fused_computation | loop fusion | flops 393216 | bytes 1048576 | tf_op jit(solution)/shard_map/stack | solution.py:36
  26.0 3.5 %all-to-all-start.1 = ((f32[4,8,1,32,128]{4,3,1,2,0:T(8,128)}), f32[4,8,1,32,128]{4,3,1,2,0:T(8,128)S(1)}, u32[]{:S(2)}, u32[]{:S(2)}) async-start(f32[4,8,1,32,128]{4,3,1,2,0:T(8,128)} %pad_maximum_fusion), calls=%async_computation.1 | async-start | bytes 1048576 | tf_op jit(solution)/shard_map/all_to_all | solution.py:35
  29.5 0.1 dynamic-slice_compare_fusion
  29.6 8.7 %all-to-all-done.1 = f32[4,8,1,32,128]{4,3,1,2,0:T(8,128)S(1)} async-done(((f32[4,8,1,32,128]{4,3,1,2,0:T(8,128)}), f32[4,8,1,32,128]{4,3,1,2,0:T(8,128)S(1)}, u32[]{:S(2)}, u32[]{:S(2)}) %all-to-all-start.1) | async-done | bytes 524320 | tf_op jit(solution)/shard_map/all_to_all | solution.py:35
  38.3 0.3 select_reduce_fusion.1
  38.6 5.8 %pmax.7 = f32[2,8,1]{1,2,0:T(1,128)S(1)} all-reduce(f32[2,8,1]{1,2,0:T(1,128)S(1)} %pad_maximum_fusion.1), channel_id=1, replica_groups=mesh['lat'=8,'lon'=4] {'lon'}, use_global_device_ids=true, to_apply=%region_4.5 | all-reduce | flops 16 | bytes 128 | tf_op jit(solution)/shard_map/pmax | solution.py:51
  44.3 0.3 copy.19
  44.7 0.8 %copy.20 = f32[8,1,32,512]{3,2,1,0:T(8,128)} copy(f32[8,1,32,512]{3,1,2,0:T(1,128)S(1)} %bitcast.19) | data formatting | bytes 1048576
  45.5 0.6 %pad_maximum_fusion.2 = f32[2,8,1]{1,2,0:T(1,128)} fusion(f32[1,8,1]{1,2,0:T(1,128)S(1)} %get-tuple-element.13, f32[1,8,1]{1,2,0:T(1,128)S(1)} %get-tuple-element.12), kind=kLoop, calls=%fused_computation.17 | loop fusion | flops 16 | bytes 128 | tf_op jit(solution)/shard_map/stack | solution.py:52
  (4 shorter events, 0.1 us)
Async XLA Ops:
  0.6 0.7 %copy-start = (s32[128,4]{0,1:T(4,128)S(1)}, s32[128,4]{0,1:T(4,128)}, u32[]{:S(2)}) copy-start(s32[128,4]{0,1:T(4,128)} %param.7) | copy-start | bytes 6148
  1.3 0.7 %copy-start.1 = (f32[16]{0:T(128)S(1)}, f32[16]{0:T(128)}, u32[]{:S(2)}) copy-start(f32[16]{0:T(128)} %param.8) | copy-start | bytes 196
  1.3 0.7 %copy-start.2 = (s32[8]{0:T(128)S(1)}, s32[8]{0:T(128)}, u32[]{:S(2)}) copy-start(s32[8]{0:T(128)} %param.10) | copy-start | bytes 100
  1.3 0.7 %copy-start.3 = (f32[16]{0:T(128)S(1)}, f32[16]{0:T(128)}, u32[]{:S(2)}) copy-start(f32[16]{0:T(128)} %param.9) | copy-start | bytes 196
  1.3 0.7 %copy-start.4 = (s32[8]{0:T(128)S(1)}, s32[8]{0:T(128)}, u32[]{:S(2)}) copy-start(s32[8]{0:T(128)} %param.11) | copy-start | bytes 100
  26.0 12.3 %all-to-all-start.1 = ((f32[4,8,1,32,128]{4,3,1,2,0:T(8,128)}), f32[4,8,1,32,128]{4,3,1,2,0:T(8,128)S(1)}, u32[]{:S(2)}, u32[]{:S(2)}) async-start(f32[4,8,1,32,128]{4,3,1,2,0:T(8,128)} %pad_maximum_fusion), calls=%async_computation.1 | async-start | bytes 1048576 | tf_op jit(solution)/shard_map/all_to_all | solution.py:35
